TPU v7x, 256 devices: a whole 4x4x8 slice. The times are simulated.
256 devices in a mesh: expert: 16 (over z, core), hidden: 16 (over x, y).
Axes of the slice: x: 4, y: 4, z: 8, core: 2. Of those that a mesh axis runs over, the one named last changes fastest.
Arguments:
- inputs: bfloat16 [3072, 2880], P('expert', 'hidden'), may hold values from -6 to 6
- out_grad: bfloat16 [3072, 2880], P('expert', 'hidden'), may hold values from -6 to 6
- expert_ids: int32 [3072, 4], P('expert'), may hold values from 0 to 15, all different within a row; in each aligned block of 192 rows (0 to 191, 192 to 383, ...) at most 72 rows name the same one
- route_weight: float32 [3072, 4], P('expert'), may hold values from 0.1 to 1
- w_gate: bfloat16 [16, 2880, 2880], P('expert', 'hidden'), may hold values from -0.109375 to 0.109375
- w_up: bfloat16 [16, 2880, 2880], P('expert', 'hidden'), may hold values from -0.109375 to 0.109375
- w_down: bfloat16 [16, 2880, 2880], P('expert', 'hidden'), may hold values from -0.109375 to 0.109375
Outputs:
- grad_input: bfloat16 [3072, 2880], P('expert', 'hidden')
- grad_route: float32 [3072, 4], P('expert')
- grad_gate: float32 [16, 2880, 2880], P('expert', 'hidden')
- grad_up: float32 [16, 2880, 2880], P('expert', 'hidden')
- grad_down: float32 [16, 2880, 2880], P('expert', 'hidden')
Inputs may be any that keep to these rules, and one draw needn't show every extreme that they name: `expert_ids`: each token names 4 different experts. Among the 192 tokens of one index of the expert axis no expert is named more than 72 times, a bound that some block reaches.
All inputs are finite; a program needn't handle non-finite values.
Results may differ from a plain program's by a relative error of at most 0.018.
Values may be sent and summed in bfloat16 or wider, within the bound.
A program may use at most 128 MiB of HBM per device.

v0:
```python
import math

import jax
import jax.numpy as jnp
from jax import lax
from jax.sharding import Mesh
from jax.sharding import PartitionSpec as P

HIDDEN = ("hidden_0", "hidden_1")


def rows_first(arrays, axis, dims):
    turned = [jnp.moveaxis(a, dim, 0) for a, dim in zip(arrays, dims)]
    both = jnp.concatenate([t.reshape(len(t), -1) for t in turned], axis=1)
    filled, at, finished = (lax.all_gather(both, axis, axis=0, tiled=True), 0, [])
    for t, dim in zip(turned, dims):
        piece = filled[:, at : at + t[0].size].reshape(-1, *t.shape[1:])
        finished.append(jnp.moveaxis(piece, 0, dim))
        at += t[0].size
    return tuple(finished)


def over_axes(value, axes):
    for axis in axes:
        value = lax.psum(value, axis)
    return value


def summed_rows(value, axes, dim):
    if not axes:
        return value
    nearer = lax.psum_scatter(value, axes[0], scatter_dimension=dim, tiled=True)
    return summed_rows(nearer, axes[1:], dim)


def in_one_piece(arrays, axis, split_dim, concat_dim, along):
    widths = [math.prod(a.shape[along:]) for a in arrays]
    both = jnp.concatenate(
        [a.reshape(*a.shape[:along], w) for a, w in zip(arrays, widths)], axis=along
    )
    filled = lax.all_to_all(both, axis, split_axis=split_dim, concat_axis=concat_dim, tiled=True)
    tiles = jnp.split(filled, [sum(widths[:k]) for k in range(1, len(widths))], axis=along)
    return tuple(
        (b.reshape(*filled.shape[:along], *a.shape[along:]) for a, b in zip(arrays, tiles))
    )


def slot_tables(expert_ids, experts, capacity):
    count, top = expert_ids.shape
    flat = expert_ids.reshape(-1)
    onehot = (flat[:, None] == jnp.arange(experts, dtype=jnp.int32)[None, :]).astype(jnp.int32)
    position = jnp.cumsum(onehot, axis=0) - 1
    slot = jnp.sum(onehot * position, axis=1)
    dest = flat * capacity + slot
    table = (
        jnp.zeros((experts * capacity,), jnp.int32)
        .at[dest]
        .set(jnp.arange(count * top, dtype=jnp.int32))
    )
    filled = jnp.zeros((experts * capacity,), jnp.int32).at[dest].set(1)
    return (dest, table, filled)


def pack_rows(values, table, filled, top, experts, capacity):
    picked = values[table // top] * filled.astype(values.dtype)[:, None]
    return picked.reshape(experts, capacity, values.shape[1])


def to_local(buffer, n_groups, local_count):
    rest = buffer.shape[2:]
    shaped = buffer.reshape((n_groups, local_count, buffer.shape[1]) + rest)
    return jnp.swapaxes(shaped, 0, 1).reshape((local_count, n_groups * buffer.shape[1]) + rest)


def from_local(buffer, n_groups, capacity):
    local_count = buffer.shape[0]
    rest = buffer.shape[2:]
    shaped = buffer.reshape((local_count, n_groups, capacity) + rest)
    return jnp.swapaxes(shaped, 0, 1).reshape((n_groups * local_count, capacity) + rest)


def per_device(inputs, out_grad, expert_ids, route_weight, w_gate, w_up, w_down):
    n_groups = lax.axis_size("expert")
    local_count = w_gate.shape[0]
    experts = local_count * n_groups
    tok_count, top = expert_ids.shape
    capacity = 3 * top * tok_count // (2 * experts)
    dest, table, filled = slot_tables(expert_ids, experts, capacity)
    send_weight = (route_weight.reshape(-1)[table] * filled.astype(jnp.float32)).reshape(
        experts, capacity
    )
    send_x = pack_rows(inputs, table, filled, top, experts, capacity)
    send_dy = pack_rows(out_grad, table, filled, top, experts, capacity)
    got_x, got_dy, got_weight = (
        lax.all_to_all(send_x, "expert", split_axis=0, concat_axis=0, tiled=True),
        lax.all_to_all(send_dy, "expert", split_axis=0, concat_axis=0, tiled=True),
        lax.all_to_all(
            send_weight.astype(jnp.bfloat16), "expert", split_axis=0, concat_axis=0, tiled=True
        ).astype(send_weight.dtype),
    )
    rows_x, rows_dy = rows_first((got_x, got_dy), HIDDEN, (2, 2))
    xs = to_local(rows_x, n_groups, local_count)
    dys = to_local(rows_dy, n_groups, local_count)
    weights = to_local(got_weight, n_groups, local_count)
    gate = jnp.einsum("esd,efd->esf", xs, w_gate, preferred_element_type=jnp.float32)
    up = jnp.einsum("esd,efd->esf", xs, w_up, preferred_element_type=jnp.float32)
    sig = jax.nn.sigmoid(gate)
    act = gate * sig
    hidden = (act * up).astype(jnp.bfloat16)
    back = jnp.einsum("esd,efd->esf", dys, w_down, preferred_element_type=jnp.float32)
    route_part = jnp.sum(hidden.astype(jnp.float32) * back, axis=2)
    grad_hidden = weights[:, :, None] * back
    scaled = (weights[:, :, None] * dys.astype(jnp.float32)).astype(jnp.bfloat16)
    grad_down = jnp.einsum("esf,esd->efd", hidden, scaled, preferred_element_type=jnp.float32)
    d_gate = (grad_hidden * up * sig * (1.0 + gate * (1.0 - sig))).astype(jnp.bfloat16)
    d_up = (grad_hidden * act).astype(jnp.bfloat16)
    grad_gate = jnp.einsum("esf,esd->efd", d_gate, xs, preferred_element_type=jnp.float32)
    grad_up = jnp.einsum("esf,esd->efd", d_up, xs, preferred_element_type=jnp.float32)
    partial_value = jnp.einsum("esf,efd->esd", d_gate, w_gate, preferred_element_type=jnp.float32)
    partial_value = partial_value + jnp.einsum(
        "esf,efd->esd", d_up, w_up, preferred_element_type=jnp.float32
    )
    route_total = over_axes(route_part, HIDDEN)
    route_back = from_local(route_total, n_groups, capacity)
    summed = summed_rows(partial_value.astype(jnp.bfloat16), HIDDEN, 2).astype(jnp.float32)
    back_rows, back_route = tuple(
        (
            part.astype(jnp.float32)
            for part in in_one_piece(
                (
                    from_local(summed, n_groups, capacity).astype(jnp.bfloat16),
                    route_back.astype(jnp.bfloat16),
                ),
                "expert",
                0,
                0,
                2,
            )
        )
    )
    per_pair = back_rows.reshape(experts * capacity, back_rows.shape[2])[dest]
    grad_input = jnp.sum(per_pair.reshape(tok_count, top, per_pair.shape[1]), axis=1).astype(
        jnp.bfloat16
    )
    grad_route = back_route.reshape(-1)[dest].reshape(tok_count, top)
    return (grad_input, grad_route, grad_gate, grad_up, grad_down)


def solution(mesh):
    torus = Mesh(
        mesh.devices.reshape(mesh.shape["expert"], 4, 4), ("expert", "hidden_0", "hidden_1")
    )
    placed = (
        P("expert", HIDDEN),
        P("expert", HIDDEN),
        P("expert", None),
        P("expert", None),
        P("expert", HIDDEN, None),
        P("expert", HIDDEN, None),
        P("expert", HIDDEN, None),
    )
    return jax.shard_map(
        per_device,
        mesh=torus,
        in_specs=placed,
        out_specs=(
            P("expert", HIDDEN),
            P("expert", None),
            P("expert", HIDDEN, None),
            P("expert", HIDDEN, None),
            P("expert", HIDDEN, None),
        ),
        check_vma=False,
    )
```

profile of v0, /device:TPU:1, one launch (start us, length us, event | category | flops | bytes accessed | tf_op | source)
XLA Modules:
  0.0 389.1 jit_solution(7536618490789103199)
XLA Ops:
  16.8 4.2 %gather_fusion.2 = bf16[1152,180]{1,0:T(8,128)(2,1)S(1)} fusion(bf16[192,180]{1,0:T(8,128)(2,1)S(1)} %copy.57, s32[2048]{0:T(1024)S(1)} %get-tuple-element.35), kind=kCustom, calls=%fused_computation.2 | custom fusion | bytes 834048 | tf_op jit(solution)/shard_map/gather | solution.py:65
  21.1 4.2 %gather_fusion.1 = bf16[1152,180]{1,0:T(8,128)(2,1)S(1)} fusion(bf16[192,180]{1,0:T(8,128)(2,1)S(1)} %copy.56, s32[2048]{0:T(1024)S(1)} %get-tuple-element.35), kind=kCustom, calls=%fused_computation.1 | custom fusion | bytes 834048 | tf_op jit(solution)/shard_map/gather | solution.py:65
  29.0 28.7 %all_to_all.21 = bf16[16,72,180]{2,1,0:T(8,128)(2,1)S(1)} all-to-all(bf16[16,72,180]{2,1,0:T(8,128)(2,1)S(1)} %get-tuple-element.33), channel_id=1, replica_groups=mesh['expert'=16,'hidden_0'=4,'hidden_1'=4] {'expert'}, dimensions={0} | all-to-all | bytes 829440 | tf_op jit(solution)/shard_map/all_to_all | solution.py:95
  57.7 21.6 %all_to_all.22 = bf16[16,72,180]{2,1,0:T(8,128)(2,1)S(1)} all-to-all(bf16[16,72,180]{2,1,0:T(8,128)(2,1)S(1)} %get-tuple-element.34), channel_id=1, replica_groups=mesh['expert'=16,'hidden_0'=4,'hidden_1'=4] {'expert'}, dimensions={0} | all-to-all | bytes 829440 | tf_op jit(solution)/shard_map/all_to_all | solution.py:96
  81.1 4.6 %gather_fusion = f32[1152]{0:T(1024)S(1)} fusion(f32[768]{0:T(1024)S(1)} %reshape.233, s32[2048]{0:T(1024)S(1)} %get-tuple-element.36), kind=kCustom, calls=%fused_computation | custom fusion | bytes 13824 | tf_op jit(solution)/shard_map/gather | solution.py:89
  85.8 9.6 %all_to_all.23 = bf16[16,1,72]{2,1,0:T(2,128)(2,1)S(1)} all-to-all(bf16[16,1,72]{2,1,0:T(2,128)(2,1)S(1)} %convert_element_type.129), channel_id=1, replica_groups=mesh['expert'=16,'hidden_0'=4,'hidden_1'=4] {'expert'}, dimensions={0} | all-to-all | bytes 4608 | tf_op jit(solution)/shard_map/all_to_all | solution.py:97
  95.5 81.5 %all-gather.3.cloned.1.call-done = bf16[16,180,2304]{2,1,0:T(8,128)(2,1)} async-done(((bf16[1,180,2304]{2,1,0:T(8,128)(2,1)}), bf16[16,180,2304]{2,1,0:T(8,128)(2,1)}) %all-gather.3.cloned.1.call-update) | async-done | bytes 13271056 | tf_op jit(solution)/shard_map/all_gather | solution.py:15
  177.0 12.6 %reshape.312 = bf16[2880,2304]{1,0:T(8,128)(2,1)} reshape(bf16[16,180,2304]{2,1,0:T(8,128)(2,1)} %all-gather.3.cloned.1.call-done) | data formatting | bytes 26542080
  189.6 10.5 %fusion.40 = (bf16[2880,1152]{1,0:T(8,128)(2,1)}, bf16[2880,1152]{1,0:T(8,128)(2,1)}) fusion(bf16[2880,2304]{1,0:T(8,128)(2,1)} %reshape.312), kind=kLoop, calls=%fused_computation.76 | loop fusion | bytes 26542080 | tf_op jit(solution)/shard_map/slice | solution.py:17
  200.1 10.1 %copy.60 = bf16[2880,1152]{0,1:T(8,128)(2,1)} copy(bf16[2880,1152]{1,0:T(8,128)(2,1)} %get-tuple-element.27) | data formatting | bytes 13271040 | tf_op jit(solution)/shard_map/slice | solution.py:17
  210.2 6.4 %fusion.11 = f32[1152,180]{0,1:T(8,128)} fusion(bf16[2880,1152]{0,1:T(8,128)(2,1)} %copy.60, bf16[1,180,2880]{2,1,0:T(8,128)(2,1)S(1)} %copy-done), kind=kOutput, calls=%fused_computation.19 | convolution fusion | flops 1194393600 | bytes 8501760 | tf_op jit(solution)/shard_map/esd,efd->esf/dot_general | solution.py:105
  220.0 10.0 %copy.59 = bf16[2880,1152]{0,1:T(8,128)(2,1)} copy(bf16[2880,1152]{1,0:T(8,128)(2,1)} %get-tuple-element.28) | data formatting | bytes 13271040 | tf_op jit(solution)/shard_map/slice | solution.py:17
  230.0 6.2 %multiply_reduce_fusion = (f32[1152]{0:T(1024)S(1)}, bf16[1152,180]{0,1:T(8,128)(2,1)S(1)}, bf16[1152,180]{0,1:T(8,128)(2,1)S(1)}, bf16[1152,180]{0,1:T(8,128)(2,1)S(1)}) fusion(f32[1152,180]{0,1:T(8,128)} %fusion.13, f32[1152,180]{0,1:T(8,128)} %fusion.11, f32[1152]{0:T(1024)S(1)} %reshape.248, bf16[1,180,2880]{2,1,0:T(8,128)(2,1)} %param.13, ...), kind=kOutput, calls=%fused_computation.34 | convolution fusion | flops 1198332288 | bytes 10584576 | tf_op jit(solution)/shard_map/esd,efd->esf/dot_general | solution.py:110
  238.4 5.0 %fusion.2 = bf16[1,1152,2880]{1,2,0:T(8,128)(2,1)} fusion(f32[1152,2880]{0,1:T(8,128)S(1)} %fusion.23, bf16[1152,180]{0,1:T(8,128)(2,1)S(1)} %get-tuple-element.30, bf16[1,180,2880]{2,1,0:T(8,128)(2,1)S(1)} %copy-done.3), kind=kOutput, calls=%fused_computation.10 | convolution fusion | flops 1201029120 | bytes 21358080 | tf_op jit(solution)/shard_map/esf,efd->esd/dot_general | solution.py:120
  245.3 4.7 %fusion.22 = f32[1,180,2880]{2,1,0:T(8,128)S(1)} fusion(bf16[1152,180]{0,1:T(8,128)(2,1)S(1)} %get-tuple-element.26, bf16[2880,1152]{0,1:T(8,128)(2,1)} %copy.59, f32[1152]{0:T(1024)S(1)} %reshape.248), kind=kOutput, calls=%fused_computation.26 | convolution fusion | flops 1204346880 | bytes 9128448 | tf_op jit(solution)/shard_map/esf,esd->efd/dot_general | solution.py:114
  250.0 3.5 copy.67
  253.5 9.9 %psum.14 = f32[1,1152]{1,0:T(1,128)S(1)} all-reduce(f32[1,1152]{1,0:T(1,128)S(1)} %reduce_sum.34), channel_id=1, replica_groups=mesh['expert'=16,'hidden_0'=4,'hidden_1'=4] {'hidden_0'}, use_global_device_ids=true, to_apply=%region_8.9 | all-reduce | flops 1152 | bytes 9216 | tf_op jit(solution)/shard_map/psum | solution.py:25
  263.4 12.9 %psum.15 = bf16[1,1152]{1,0:T(2,128)(2,1)S(1)} all-reduce(f32[1,1152]{1,0:T(1,128)S(1)} %psum.14), channel_id=1, replica_groups=mesh['expert'=16,'hidden_0'=4,'hidden_1'=4] {'hidden_1'}, use_global_device_ids=true, to_apply=%region_9.10 | all-reduce | flops 1152 | bytes 6912 | tf_op jit(solution)/shard_map/psum | solution.py:25
  276.3 36.8 %reduce-scatter.5.cloned.1.call-done = bf16[1,1152,720]{1,2,0:T(8,128)(2,1)} async-done(((bf16[1,1152,2880]{1,2,0:T(8,128)(2,1)}), bf16[1,1152,720]{1,2,0:T(8,128)(2,1)}) %reduce-scatter.5.cloned.1.call-update) | async-done | bytes 1658896 | tf_op jit(solution)/shard_map/reduce_scatter | solution.py:32
  313.2 26.3 %fusion = bf16[1152,192]{0,1:T(8,128)(2,1)S(1)} fusion(bf16[1,1152,720]{1,2,0:T(8,128)(2,1)} %reduce-scatter.5.cloned.1.call-done), kind=kCustom, calls=%all-reduce-scatter | all-reduce-scatter fusion | flops 884737 | bytes 2102272
  344.5 9.7 %all-to-all-start.3 = ((bf16[16,72,181]{2,1,0:T(8,128)(2,1)}), bf16[16,72,181]{2,1,0:T(8,128)(2,1)S(1)}, u32[]{:S(2)}, u32[]{:S(2)}) async-start(bf16[16,72,181]{2,1,0:T(8,128)(2,1)} %pad_maximum_fusion), calls=%async_computation.4 | async-start | bytes 1179648 | tf_op jit(solution)/shard_map/all_to_all | solution.py:41
  354.2 4.6 %fusion.19 = f32[1,180,2880]{2,1,0:T(8,128)S(1)} fusion(bf16[1152,180]{0,1:T(8,128)(2,1)S(1)} %get-tuple-element.30, bf16[2880,1152]{0,1:T(8,128)(2,1)} %copy.60), kind=kOutput, calls=%fused_computation.25 | convolution fusion | flops 1194393600 | bytes 9123840 | tf_op jit(solution)/shard_map/esf,esd->efd/dot_general | solution.py:118
  362.3 4.6 %fusion.16 = f32[1,180,2880]{2,1,0:T(8,128)S(1)} fusion(bf16[1152,180]{0,1:T(8,128)(2,1)S(1)} %get-tuple-element.29, bf16[2880,1152]{0,1:T(8,128)(2,1)} %copy.60), kind=kOutput, calls=%fused_computation.24 | convolution fusion | flops 1194393600 | bytes 9123840 | tf_op jit(solution)/shard_map/esf,esd->efd/dot_general | solution.py:117
  377.0 4.5 %gather_fusion.4 = f32[768]{0:T(1024)S(1)} fusion(f32[1152]{0:T(1024)S(1)} %reshape.251, s32[1024]{0:T(1024)S(1)} %pad_clamp_fusion.2), kind=kCustom, calls=%fused_computation.4 | custom fusion | bytes 9216 | tf_op jit(solution)/shard_map/gather | solution.py:145
  (73 shorter events, 41.4 us)
Async XLA Ops:
  7.2 203.0 %copy-start = (bf16[1,180,2880]{2,1,0:T(8,128)(2,1)S(1)}, bf16[1,180,2880]{2,1,0:T(8,128)(2,1)}, u32[]{:S(2)}) copy-start(bf16[1,180,2880]{2,1,0:T(8,128)(2,1)} %param.11) | copy-start | bytes 3110404
  7.2 169.8 %all-gather.3.cloned.1.call-start = ((), (), s32[]{:S(2)}) async-start(), calls=%async_computation.6 | async-start | bytes 14413824 | tf_op jit(solution)/shard_map/all_gather | solution.py:15
  79.3 1.6 copy-start.4
  80.8 232.4 %reduce-scatter.5.cloned.1.call-start = ((), (), s32[]{:S(2)}) async-start(), calls=%async_computation.5 | async-start | bytes 8294400 | tf_op jit(solution)/shard_map/reduce_scatter | solution.py:32
  210.2 6.4 %copy-start.2 = (bf16[2880,1152]{0,1:T(8,128)(2,1)S(1)}, bf16[2880,1152]{0,1:T(8,128)(2,1)}, u32[]{:S(2)}) copy-start(bf16[2880,1152]{0,1:T(8,128)(2,1)} %copy.60) | copy-start | bytes 19906564
  210.2 6.4 %copy-start.3 = (bf16[1,180,2880]{2,1,0:T(8,128)(2,1)S(1)}, bf16[1,180,2880]{2,1,0:T(8,128)(2,1)}, u32[]{:S(2)}) copy-start(bf16[1,180,2880]{2,1,0:T(8,128)(2,1)} %param.12) | copy-start | bytes 3110404
  243.4 0.7 copy-start.5
  339.5 2.9 collective-permute-start
  344.5 28.3 %all-to-all-start.3 = ((bf16[16,72,181]{2,1,0:T(8,128)(2,1)}), bf16[16,72,181]{2,1,0:T(8,128)(2,1)S(1)}, u32[]{:S(2)}, u32[]{:S(2)}) async-start(bf16[16,72,181]{2,1,0:T(8,128)(2,1)} %pad_maximum_fusion), calls=%async_computation.4 | async-start | bytes 1179648 | tf_op jit(solution)/shard_map/all_to_all | solution.py:41
  375.8 6.4 %copy-start.1 = (bf16[1,180,2880]{2,1,0:T(8,128)(2,1)S(1)}, bf16[1,180,2880]{2,1,0:T(8,128)(2,1)}, u32[]{:S(2)}) copy-start(bf16[1,180,2880]{2,1,0:T(8,128)(2,1)} %param.11) | copy-start | bytes 3110404
Sparse Core Ops, SparseCore 0:
  80.9 96.0 all-gather.2
  243.5 69.5 reduce-scatter.4
where the time goes:
time: 390 us; the launch traced here: 389 us
  waiting for transfers between devices  122 us (31%)
  blocking collectives  109 us (28%)
  local copies, waits for them, and re-layouts  90.1 us (23%)
  matrix products  37 us (9%)
  between operations  15.1 us (4%)
  starting transfers between devices  11.2 us (3%)
  other arithmetic  5.07 us (1%)
    all_gather x1, waiting for transfers between devices, rows_first(): lax.all_gather(both, axis, axis=0, tiled=True)  81.5 us
    reduce_scatter x1, waiting for transfers between devices, summed_rows(): nearer = lax.psum_scatter(value, axes[0], scatter_dimension=dim, tiled=True)  36.8 us
    unnamed x27, local copies, waits for them, and re-layouts  30.9 us
    slice x3, local copies, waits for them, and re-layouts, rows_first(): piece = filled[:, at:at + t[0].size].reshape(-1, *t.shape[1:])  30.6 us
    all_to_all x1, blocking collectives, per_device(): lax.all_to_all(send_x, 'expert', split_axis=0, concat_axis=0, tiled=True)  28.7 us
    unnamed x1, blocking collectives  26.3 us
    psum x2, blocking collectives, over_axes(): value = lax.psum(value, axis)  22.8 us
    all_to_all x1, blocking collectives, per_device(): lax.all_to_all(send_dy, 'expert', split_axis=0, concat_axis=0, tiled=True)  21.6 us
  transfers between devices with their start and end apart: 4, of which 4 were waited for; matrix products, arithmetic and copies ran while one was open for 8% of the time, Pallas kernels for 0%

commit v1 on v0

v1 whole, which is shorter than its diff:
```python
import jax
import jax.numpy as jnp
from jax import lax
from jax.experimental import pallas as pl
from jax.experimental.pallas import tpu as pltpu
from jax.sharding import Mesh
from jax.sharding import PartitionSpec as P

HIDDEN = ("hidden_0", "hidden_1")
BF = jnp.bfloat16
F32 = jnp.float32
TOK = 192
CAP = 72
NB = 16
SH = 180
ROWS = NB * CAP
W2 = 384
CH = 192
NC = ROWS // CH
MESH_ID = pl.DeviceIdType.MESH
NT = (((1,), (1,)), ((), ()))
TN = (((0,), (0,)), ((), ()))


def remote(src, dst, send, recv, device):
    return pltpu.make_async_remote_copy(
        src_ref=src, dst_ref=dst, send_sem=send, recv_sem=recv,
        device_id=device, device_id_type=MESH_ID,
    )


def dispatch_kernel(xd_ref, rows_ref, buf, acc, ring_send, sib_send, recv):
    e = lax.axis_index("expert")
    hx, hy = lax.axis_index("hidden_0"), lax.axis_index("hidden_1")
    z, core = e // 2, e % 2
    right = ((z + 1) % 8) * 2 + core
    left = ((z + 7) % 8) * 2 + core
    sib = z * 2 + 1 - core

    barrier = pltpu.get_barrier_semaphore()
    for peer in (right, left, sib):
        pl.semaphore_signal(barrier, inc=1, device_id=(peer, hx, hy), device_id_type=MESH_ID)
    pl.semaphore_wait(barrier, 3)

    half = TOK // 2

    def copy(step, h, block, target, send):
        rows = pl.ds(half * h, half)
        src = xd_ref.at[rows] if step == 0 else buf.at[block, rows]
        return remote(src, buf.at[block, rows], send, recv.at[block, h], (target, hx, hy))

    def origin(d):
        return ((z + d + 8) % 8) * 2 + core

    started = []

    def go(c):
        c.start()
        started.append(c)

    for h in range(2):
        go(copy(0, h, e, right, ring_send.at[0, 0, h]))
        go(copy(0, h, e, left, ring_send.at[1, 0, h]))
    for h in range(2):
        go(copy(0, h, e, sib, sib_send.at[0, h]))
    buf[e] = xd_ref[...]
    for s in range(1, 5):
        for way in range(2):
            block = origin(-s if way == 0 else s)
            for h in range(2):
                if s == 4 and h != way:
                    continue
                copy(1, h, block, right, ring_send.at[0, 0, 0]).wait_recv()
                if s < 3 or (s == 3 and h == way):
                    go(copy(1, h, block, (right, left)[way], ring_send.at[way, s, h]))
                k = s if way == 0 else 8 - s
                go(copy(1, h, block, sib, sib_send.at[k, h]))
    for d in range(8):
        block = ((z + d) % 8) * 2 + 1 - core
        for h in range(2):
            copy(1, h, block, right, ring_send.at[0, 0, 0]).wait_recv()

    lane = lax.broadcasted_iota(jnp.int32, (TOK, 128), 1)
    lower = (
        lax.broadcasted_iota(jnp.int32, (TOK, TOK), 0)
        > lax.broadcasted_iota(jnp.int32, (TOK, TOK), 1)
    ).astype(BF)
    ones = jnp.ones((128, 128), BF)
    ef = e.astype(F32)

    def one_block(b, carry):
        blk = buf[b]
        meta = blk[:, 128:256].astype(F32)
        hit = ((meta == ef) & (lane >= 52) & (lane < 56)).astype(F32).astype(BF)
        named = jnp.dot(hit, ones, preferred_element_type=F32)
        slot = jnp.dot(lower, named.astype(BF), preferred_element_type=F32)
        pick = ((slot == lane.astype(F32)) & (named > 0.5)).astype(F32).astype(BF)
        rows = lax.dot_general(pick, blk, TN, preferred_element_type=F32)
        acc[pl.ds(pl.multiple_of(b * CAP, 8), CAP), :] = rows[:CAP]
        return carry

    lax.fori_loop(0, NB, one_block, 0, unroll=4)
    rows_ref[...] = acc[...].astype(BF)
    for c in started:
        c.wait_send()


def dispatch(xd):
    return pl.pallas_call(
        dispatch_kernel,
        out_shape=jax.ShapeDtypeStruct((ROWS, W2), BF),
        in_specs=[pl.BlockSpec(memory_space=pltpu.VMEM)],
        out_specs=pl.BlockSpec(memory_space=pltpu.VMEM),
        scratch_shapes=[
            pltpu.VMEM((NB, TOK, W2), BF),
            pltpu.VMEM((ROWS, W2), F32),
            pltpu.SemaphoreType.DMA((2, 4, 2)),
            pltpu.SemaphoreType.DMA((8, 2)),
            pltpu.SemaphoreType.DMA((NB, 2)),
        ],
        compiler_params=pltpu.CompilerParams(
            collective_id=0, has_side_effects=True, vmem_limit_bytes=24 * 2**20
        ),
        name="dispatch",
    )(xd)


def expert_kernel(
    rows_ref, wg_ref, wu_ref, wd_ref,
    gg_ref, gu_ref, gd_ref, out_ref, route_ref,
    xd, wraw, wf, wb, part, fwd, near, quart, gsum, term, dgu_t, hw_t, rp, rp_all,
    w_sem, ag_send, ag_recv, rs_send, rs_recv, rt_send, rt_recv,
):
    e = lax.axis_index("expert")
    hx, hy = lax.axis_index("hidden_0"), lax.axis_index("hidden_1")
    me = hx * 4 + hy

    def peer(j):
        return (e, j // 4, j % 4)

    barrier = pltpu.get_barrier_semaphore()
    for d in range(1, NB):
        pl.semaphore_signal(barrier, inc=1, device_id=peer((me + d) % NB), device_id_type=MESH_ID)
    raw = [wg_ref, wu_ref, wd_ref]
    load = [pltpu.make_async_copy(raw[k], wraw.at[k % 2], w_sem.at[k]) for k in range(3)]
    load[0].start()
    load[1].start()
    pl.semaphore_wait(barrier, NB - 1)

    def place(c):
        odd = c % 2
        a = jnp.where(odd == 0, hx, hy)
        b = jnp.where(odd == 0, hy, hx)
        return odd, a, b

    def shard(odd, a, b):
        return jnp.where(odd == 0, a * 4 + b, b * 4 + a)

    def rows_of(c):
        return pl.ds(pl.multiple_of(c * CH, CH), CH)

    def ag(c, slot, to, k, own=False):
        src = rows_ref.at[rows_of(c)] if own else xd.at[slot, rows_of(c)]
        return remote(
            src, xd.at[slot, rows_of(c)], ag_send.at[c, k], ag_recv.at[c, slot], peer(to)
        )

    def ag_wait(c, slot):
        ag(c, slot, me, 0).wait_recv()

    def stage_a(c):
        odd, a, b = place(c)
        ag(c, me, shard(odd, (a + 1) % 4, b), 0, True).start()
        ag(c, me, shard(odd, (a + 3) % 4, b), 1, True).start()
        ag(c, me, shard(odd, a, (b + 1) % 4), 3, True).start()
        ag(c, me, shard(odd, a, (b + 3) % 4), 4, True).start()

    def stage_b(c):
        odd, a, b = place(c)
        from_left = shard(odd, (a + 3) % 4, b)
        from_right = shard(odd, (a + 1) % 4, b)
        flip = (c // 2) % 2
        ag_wait(c, from_left)
        ag_wait(c, from_right)
        ag(
            c, jnp.where(flip == 0, from_left, from_right),
            jnp.where(flip == 0, from_right, from_left), 2,
        ).start()
        up, down = shard(odd, a, (b + 1) % 4), shard(odd, a, (b + 3) % 4)
        ag(c, from_left, up, 5).start()
        ag(c, from_left, down, 6).start()
        ag(c, from_right, up, 7).start()
        ag(c, from_right, down, 8).start()

    def stage_c(c):
        odd, a, b = place(c)
        far = shard(odd, (a + 2) % 4, b)
        up, down = shard(odd, a, (b + 1) % 4), shard(odd, a, (b + 3) % 4)
        ag_wait(c, far)
        ag(c, far, up, 9).start()
        ag(c, far, down, 10).start()
        for k, da in ((11, 0), (12, 1)):
            slot = shard(odd, (a + da) % 4, (b + 3) % 4)
            ag_wait(c, slot)
            ag(c, slot, up, k).start()
        slot = shard(odd, (a + 3) % 4, (b + 1) % 4)
        ag_wait(c, slot)
        ag(c, slot, down, 13).start()

    def stage_d(c):
        odd, a, b = place(c)
        slot = shard(odd, (a + 2) % 4, (b + 1) % 4)
        ag_wait(c, slot)
        ag(c, slot, shard(odd, a, (b + 3) % 4), 14).start()

    def rs(c, src, dst, k, to):
        return remote(src, dst, rs_send.at[c, k], rs_recv.at[c, k], peer(to))

    def rs_copy(c, k):
        odd, a, b = place(c)
        right, left = shard(odd, (a + 1) % 4, b), shard(odd, (a + 3) % 4, b)
        up, down = shard(odd, a, (b + 1) % 4), shard(odd, a, (b + 3) % 4)
        ar, al, ao = (a + 1) % 4, (a + 3) % 4, (a + 2) % 4
        bu, bd, bo = (b + 1) % 4, (b + 3) % 4, (b + 2) % 4
        if k == 0:
            return rs(c, part.at[c, ao, 0], fwd.at[c, 0], k, right)
        if k == 1:
            return rs(c, part.at[c, ao, 1], fwd.at[c, 1], k, left)
        if k == 2:
            return rs(c, part.at[c, ar, 1], near.at[c, 0, 1], k, right)
        if k == 3:
            return rs(c, part.at[c, al, 0], near.at[c, 1, 0], k, left)
        if k == 4:
            return rs(c, part.at[c, ar, 0], near.at[c, 0, 0], k, right)
        if k == 5:
            return rs(c, part.at[c, al, 1], near.at[c, 1, 1], k, left)
        flip = (c // 2) % 2
        ahead, behind = jnp.where(flip == 0, up, down), jnp.where(flip == 0, down, up)
        ba, bb = jnp.where(flip == 0, bu, bd), jnp.where(flip == 0, bd, bu)
        if k == 6:
            return rs(c, quart.at[c, bo], gsum.at[c], k, ahead)
        if k == 7:
            return rs(c, quart.at[c, bb], term.at[c, 0], k, behind)
        return rs(c, quart.at[c, ba], term.at[c, 1], k, ahead)

    def stage_e(c):
        odd, a, b = place(c)
        rows = rows_of(c)
        bo = (b + 2) % 4
        for da in range(4):
            ag_wait(c, shard(odd, (a + da) % 4, bo))
        ag_wait(c, shard(odd, (a + 2) % 4, (b + 3) % 4))
        ag_wait(c, shard(odd, (a + 3) % 4, (b + 3) % 4))
        ag_wait(c, shard(odd, a, (b + 1) % 4))
        ag_wait(c, shard(odd, (a + 1) % 4, (b + 1) % 4))

        gate = up = back = None
        for s in range(NB):
            x = xd[s, rows, 0:256]
            y = xd[s, rows, 128:384]
            g1 = lax.dot_general(x, wf[0, s], NT, preferred_element_type=F32)
            u1 = lax.dot_general(x, wf[1, s], NT, preferred_element_type=F32)
            b1 = lax.dot_general(y, wf[2, s], NT, preferred_element_type=F32)
            gate = g1 if gate is None else gate + g1
            up = u1 if up is None else up + u1
            back = b1 if back is None else back + b1
        meta = xd[0, rows, 128:256].astype(F32)
        lane = lax.broadcasted_iota(jnp.int32, (CH, 128), 1)
        whole = pltpu.roll(meta, 124, 1) + pltpu.roll(meta, 120, 1)
        mine = (meta == e.astype(F32)) & (lane >= 52) & (lane < 56)
        w = jnp.sum(jnp.where(mine, whole, 0.0), axis=1, keepdims=True)
        sig = jax.nn.sigmoid(gate)
        act = gate * sig
        prod = act * up
        gh = w * back
        d_gate = gh * up * sig * (1.0 + gate * (1.0 - sig))
        d_up = gh * act
        hb = prod.astype(BF).astype(F32) * back
        hi = hb.astype(BF)
        lo = (hb - hi.astype(F32)).astype(BF)
        row8 = (lax.broadcasted_iota(jnp.int32, (8, CH), 0) == c).astype(F32).astype(BF)
        rp[:, 0:CH] += lax.dot_general(
            row8, hi, NT, preferred_element_type=F32
        ) + lax.dot_general(row8, lo, NT, preferred_element_type=F32)
        dgb, dub = d_gate.astype(BF), d_up.astype(BF)
        dgu_t[c, 0:192, :] = d_gate.T.astype(BF)
        dgu_t[c, 192:384, :] = d_up.T.astype(BF)
        hw_t[c] = (w * prod).T.astype(BF)
        for q in range(4):
            for h in range(2):
                lanes = slice(768 * q + 384 * h, 768 * q + 384 * h + 384)
                p = jnp.dot(dgb, wb[odd, 0, :, lanes], preferred_element_type=F32) + jnp.dot(
                    dub, wb[odd, 1, :, lanes], preferred_element_type=F32
                )
                part[c, q, h] = p.astype(BF)
        for k in range(4):
            rs_copy(c, k).start()

    def stage_f(c):
        odd, a, b = place(c)
        ar, al = (a + 1) % 4, (a + 3) % 4
        rs_copy(c, 0).wait_recv()
        part[c, ar, 0] = (part[c, ar, 0].astype(F32) + fwd[c, 0].astype(F32)).astype(BF)
        rs_copy(c, 4).start()
        rs_copy(c, 1).wait_recv()
        part[c, al, 1] = (part[c, al, 1].astype(F32) + fwd[c, 1].astype(F32)).astype(BF)
        rs_copy(c, 5).start()

    def stage_g(c):
        odd, a, b = place(c)
        for k in (2, 3, 4, 5):
            rs_copy(c, k).wait_recv()
        for h in range(2):
            q = (
                part[c, a, h].astype(F32) + near[c, 0, h].astype(F32) + near[c, 1, h].astype(F32)
            ).astype(BF)
            quart[c, 2 * h] = q[:, 0:256]
            quart[c, 2 * h + 1] = q[:, 128:384]
        rs_copy(c, 6).start()
        rs_copy(c, 7).start()

    def stage_h(c):
        odd, a, b = place(c)
        flip = (c // 2) % 2
        ba = jnp.where(flip == 0, (b + 1) % 4, (b + 3) % 4)
        rs_copy(c, 6).wait_recv()
        quart[c, ba] = (quart[c, ba].astype(F32) + gsum[c].astype(F32)).astype(BF)
        rs_copy(c, 8).start()

    def stage_i(c):
        odd, a, b = place(c)
        rs_copy(c, 7).wait_recv()
        rs_copy(c, 8).wait_recv()
        r = quart[c, b].astype(F32) + term[c, 0].astype(F32) + term[c, 1].astype(F32)
        r = jnp.where(b % 2 == 1, pltpu.roll(r, 192, 1), r)
        out_ref[rows_of(c), :] = r[:, 0:192].astype(BF)

    def guard(cond, f, *args):
        @pl.when(cond)
        def _():
            f(*args)

    stage_a(0)
    xd[me] = rows_ref[...]
    rp[...] = jnp.zeros_like(rp)
    wf[...] = jnp.zeros_like(wf)
    wb[...] = jnp.zeros_like(wb)
    for k in range(3):
        load[k].wait()
        for s in range(NB):
            w = wraw[k % 2, :, SH * s : SH * s + SH]
            at = 0 if k < 2 else 64
            wf[k, s, 0:SH, at : at + SH] = w
            if k < 2:
                t = (s % 4) * 4 + s // 4
                wb[0, k, 0:SH, 192 * s : 192 * s + SH] = w
                wb[1, k, 0:SH, 192 * t : 192 * t + SH] = w
        if k == 0:
            load[2].start()

    def step(t, carry):
        guard((t >= 1) & (t < NC), stage_a, t)
        guard((t >= 1) & (t < NC + 1), stage_b, t - 1)
        guard((t >= 2) & (t < NC + 2), stage_c, t - 2)
        guard((t >= 3) & (t < NC + 3), stage_d, t - 3)
        guard((t >= 5) & (t < NC + 5), stage_f, t - 5)
        guard((t >= 6) & (t < NC + 6), stage_g, t - 6)
        guard((t >= 7) & (t < NC + 7), stage_h, t - 7)
        guard((t >= 8) & (t < NC + 8), stage_i, t - 8)
        guard((t >= 4) & (t < NC + 4), stage_e, t - 4)
        return carry

    lax.fori_loop(0, NC + 4, step, 0)

    def rt(d):
        j = (me + d) % NB
        return remote(rp, rp_all.at[me], rt_send.at[d], rt_recv.at[me], peer(j))

    for d in range(1, NB):
        rt(d).start()
    rp_all[me] = rp[...]

    def weight_grads(s):
        gu = hd = None
        for c in range(NC):
            x = xd[s, CH * c : CH * c + CH, 0:256]
            y = xd[s, CH * c : CH * c + CH, 128:384]
            g1 = jnp.dot(dgu_t[c], x, preferred_element_type=F32)
            h1 = jnp.dot(hw_t[c], y, preferred_element_type=F32)
            gu = g1 if gu is None else gu + g1
            hd = h1 if hd is None else hd + h1
        lanes = slice(SH * s, SH * s + SH)
        gg_ref[:, lanes] = gu[0:SH, 0:SH]
        gu_ref[:, lanes] = gu[192 : 192 + SH, 0:SH]
        gd_ref[:, lanes] = hd[0:SH, 64 : 64 + SH]

    done = 0
    for t in range(NC + 4, NC + 8):
        for off, f in ((5, stage_f), (6, stage_g), (7, stage_h), (8, stage_i)):
            if t - off < NC:
                f(t - off)
        for s in range(done, done + 4):
            weight_grads(s)
        done += 4

    for d in range(1, NB):
        j = (me + d) % NB
        remote(rp, rp_all.at[j], rt_send.at[d], rt_recv.at[j], peer(j)).wait_recv()
    total = rp_all[0]
    for j in range(1, NB):
        total = total + rp_all[j]
    route_ref[...] = total

    for d in range(1, NB):
        rt(d).wait_send()

    def drain(c, carry):
        for k in range(15):
            ag(c, me, me, k, True).wait_send()
        for k in range(9):
            rs_copy(c, k).wait_send()
        return carry

    lax.fori_loop(0, NC, drain, 0)


def experts(rows, w_gate, w_up, w_down):
    vm = pl.BlockSpec(memory_space=pltpu.VMEM)
    hbm = pl.BlockSpec(memory_space=pl.ANY)
    grad = jax.ShapeDtypeStruct((SH, NB * SH), F32)
    return pl.pallas_call(
        expert_kernel,
        out_shape=[
            grad, grad, grad,
            jax.ShapeDtypeStruct((ROWS, 192), BF),
            jax.ShapeDtypeStruct((8, 256), F32),
        ],
        in_specs=[vm, hbm, hbm, hbm],
        out_specs=[vm] * 5,
        scratch_shapes=[
            pltpu.VMEM((NB, ROWS, W2), BF),
            pltpu.VMEM((2, SH, NB * SH), BF),
            pltpu.VMEM((3, NB, 192, 256), BF),
            pltpu.VMEM((2, 2, 192, NB * 192), BF),
            pltpu.VMEM((NC, 4, 2, CH, 384), BF),
            pltpu.VMEM((NC, 2, CH, 384), BF),
            pltpu.VMEM((NC, 2, 2, CH, 384), BF),
            pltpu.VMEM((NC, 4, CH, 256), BF),
            pltpu.VMEM((NC, CH, 256), BF),
            pltpu.VMEM((NC, 2, CH, 256), BF),
            pltpu.VMEM((NC, 384, CH), BF),
            pltpu.VMEM((NC, 192, CH), BF),
            pltpu.VMEM((8, 256), F32),
            pltpu.VMEM((NB, 8, 256), F32),
            pltpu.SemaphoreType.DMA((3,)),
            pltpu.SemaphoreType.DMA((NC, 15)),
            pltpu.SemaphoreType.DMA((NC, NB)),
            pltpu.SemaphoreType.DMA((NC, 9)),
            pltpu.SemaphoreType.DMA((NC, 9)),
            pltpu.SemaphoreType.DMA((NB,)),
            pltpu.SemaphoreType.DMA((NB,)),
        ],
        compiler_params=pltpu.CompilerParams(
            collective_id=1, has_side_effects=True, vmem_limit_bytes=67043328
        ),
        name="experts",
    )(rows, w_gate, w_up, w_down)


def per_device(inputs, out_grad, expert_ids, route_weight, w_gate, w_up, w_down):
    ids = expert_ids.astype(BF)
    w_hi = route_weight.astype(BF)
    w_lo = (route_weight - w_hi.astype(F32)).astype(BF)
    xd = jnp.concatenate(
        [inputs, ids, w_hi, w_lo, out_grad, jnp.zeros((TOK, W2 - 372), BF)], axis=1
    )
    rows = dispatch(xd)
    gg, gu, gd, back, route = experts(rows, w_gate[0], w_up[0], w_down[0])

    route = route[:NC, :CH].reshape(ROWS, 1)
    r_hi = route.astype(BF)
    r_lo = (route - r_hi.astype(F32)).astype(BF)
    send = jnp.concatenate([back[:, :SH], r_hi, r_lo], axis=1).reshape(NB, CAP, SH + 2)
    got = lax.all_to_all(send, "expert", split_axis=0, concat_axis=0, tiled=True)

    experts_ = jnp.arange(NB, dtype=jnp.int32)
    hit = expert_ids[:, :, None] == experts_[None, None, :]
    named = jnp.any(hit, axis=1).astype(F32)
    before = jnp.tril(jnp.ones((TOK, TOK), F32), -1)
    slot = jnp.dot(before, named, preferred_element_type=F32)
    at = slot[:, None, :, None] == jnp.arange(CAP, dtype=F32)[None, None, None, :]
    pick = (hit[:, :, :, None] & at).astype(BF).reshape(TOK, 4, ROWS)
    got = got.reshape(ROWS, SH + 2)
    mixed = jnp.einsum("tkr,rd->ktd", pick, got, preferred_element_type=F32)
    grad_input = jnp.sum(mixed[:, :, :SH], axis=0).astype(BF)
    grad_route = (mixed[:, :, SH] + mixed[:, :, SH + 1]).T
    return grad_input, grad_route, gg[None], gu[None], gd[None]


def solution(mesh):
    torus = Mesh(
        mesh.devices.reshape(mesh.shape["expert"], 4, 4), ("expert", "hidden_0", "hidden_1")
    )
    placed = (
        P("expert", HIDDEN),
        P("expert", HIDDEN),
        P("expert", None),
        P("expert", None),
        P("expert", HIDDEN, None),
        P("expert", HIDDEN, None),
        P("expert", HIDDEN, None),
    )
    return jax.shard_map(
        per_device,
        mesh=torus,
        in_specs=placed,
        out_specs=(
            P("expert", HIDDEN),
            P("expert", None),
            P("expert", HIDDEN, None),
            P("expert", HIDDEN, None),
            P("expert", HIDDEN, None),
        ),
        check_vma=False,
    )
```

time: 390 us -> 214 us (0.55)
  Pallas kernels: 0 us -> 176 us
  waiting for transfers between devices: 122 us -> 7.55 us
  blocking collectives: 109 us -> 0 us
  local copies, waits for them, and re-layouts: 90.1 us -> 15.9 us
  matrix products: 37 us -> 1.14 us
  between operations: 15.1 us -> 0.76 us
    pallas_call x0 -> x2, Pallas kernels: none -> 176 us  [the longest x1 144 us: experts(): pl.pallas_call(expert_kernel, out_shape=[grad, grad, grad, jax.ShapeDtype...]
    all_gather x1 -> x0, waiting for transfers between devices: 81.5 us -> none  [rows_first(): lax.all_gather(both, axis, axis=0, tiled=True)]
    all_to_all x3 -> x0, blocking collectives: 59.8 us -> none  [the longest x1 28.7 us: per_device(): lax.all_to_all(send_x, 'expert', split_axis=0, concat_axis=0, tiled=True)]
    reduce_scatter x1 -> x0, waiting for transfers between devices: 36.8 us -> none  [summed_rows(): nearer = lax.psum_scatter(value, axes[0], scatter_dimension=dim, tiled=True)]
    dot_general x8 -> x2, matrix products: 37 us -> 1.14 us  [the longest x1 0.92 us: per_device(): mixed = jnp.einsum('tkr,rd->ktd', pick, got, preferred_element_type=F32)]
    slice x4 -> x0, local copies, waits for them, and re-layouts: 30.9 us -> none  [the longest x3 30.6 us: rows_first(): piece = filled[:, at:at + t[0].size].reshape(-1, *t.shape[1:])]
    unnamed x1 -> x0, blocking collectives: 26.3 us -> none
    psum x2 -> x0, blocking collectives: 22.8 us -> none  [over_axes(): value = lax.psum(value, axis)]
  transfers between devices with their start and end apart: 4 -> 1, of which waited for: 4 -> 1; matrix products, arithmetic and copies ran while one was open for 8% -> 5% of each run, Pallas kernels for 0% -> 0%
where the time goes in v1:
time: 214 us
  Pallas kernels  176 us (82%)
  local copies, waits for them, and re-layouts  15.9 us (7%)
  starting transfers between devices  7.86 us (4%)
  waiting for transfers between devices  7.55 us (4%)
  other arithmetic  4.7 us (2%)
    pallas_call x1, Pallas kernels, experts(): pl.pallas_call(expert_kernel, out_shape=[grad, grad, grad, jax.ShapeDtype...  144 us
    pallas_call x1, Pallas kernels, dispatch(): pl.pallas_call(dispatch_kernel, out_shape=jax.ShapeDtypeStruct((ROWS, W2)...  31.9 us
    unnamed x16, local copies, waits for them, and re-layouts  14 us
    all_to_all x1, starting transfers between devices, per_device(): lax.all_to_all(send, 'expert', split_axis=0, concat_axis=0, tiled=True)  7.86 us
    all_to_all x1, waiting for transfers between devices, per_device(): lax.all_to_all(send, 'expert', split_axis=0, concat_axis=0, tiled=True)  7.55 us
  transfers between devices with their start and end apart: 1, of which 1 were waited for; matrix products, arithmetic and copies ran while one was open for 5% of the time, Pallas kernels for 0%

profile of v1, /device:TPU:1, one launch (start us, length us, event | category | flops | bytes accessed | tf_op | source)
XLA Modules:
  0.0 213.8 jit_solution(10546049661826197360)
XLA Ops:
  0.6 0.7 convert_element_type.58
  1.3 0.8 subtract_convert_fusion.1
  2.2 0.2 copy.33
  2.4 0.2 copy.34
  2.6 1.0 copy.32
  3.6 1.0 copy.36
  4.6 0.2 concatenate.9.xd_ref
  4.8 31.9 %dispatch.1.rows_ref = bf16[1152,384]{1,0:T(8,128)(2,1)S(1)} custom-call(bf16[192,384]{1,0:T(8,128)(2,1)S(1)} %concatenate.9.xd_ref), custom_call_target="tpu_custom_call" | custom-call | tf_op jit(solution)/shard_map/dispatch/pallas_call | solution.py:109
  36.7 0.9 copy-done
  37.6 143.9 %experts.1 = (f32[180,2880]{1,0:T(8,128)}, f32[180,2880]{1,0:T(8,128)}, f32[180,2880]{1,0:T(8,128)}, bf16[1152,192]{1,0:T(8,128)(2,1)}, f32[8,256]{1,0:T(8,128)}) custom-call(bf16[1152,384]{1,0:T(8,128)(2,1)} %copy-done, bf16[180,2880]{1,0:T(8,128)(2,1)} %bitcast.26, bf16[180,2880]{1,0:T(8,128)(2,1)} %bitcast.27, bf16[180,2880]{1,0:T(8,128)(2,1)} %bitcast.28), custom_call_target="tpu_custom_call" | custom-call | tf_op jit(solution)/shard_map/experts/pallas_call | solution.py:431
  181.5 0.8 reshape.71
  182.3 0.2 copy.38
  182.6 0.2 copy.37
  182.8 2.3 %pad_maximum_fusion = bf16[16,72,182]{2,1,0:T(8,128)(2,1)} fusion(bf16[16,72,1]{2,1,0:T(8,128)(2,1)S(1)} %copy.38, bf16[16,72,1]{2,1,0:T(8,128)(2,1)S(1)} %copy.37, bf16[16,72,180]{2,1,0:T(8,128)(2,1)} %bitcast.29), kind=kLoop, calls=%fused_computation.7 | loop fusion | flops 1257984 | bytes 838656 | tf_op jit(solution)/shard_map/concatenate | solution.py:483
  185.1 7.9 %all-to-all-start = ((bf16[16,72,182]{2,1,0:T(8,128)(2,1)}), bf16[16,72,182]{2,1,0:T(8,128)(2,1)S(1)}, u32[]{:S(2)}, u32[]{:S(2)}) async-start(bf16[16,72,182]{2,1,0:T(8,128)(2,1)} %pad_maximum_fusion), calls=%async_computation | async-start | bytes 1179648 | tf_op jit(solution)/shard_map/all_to_all | solution.py:484
  193.0 3.5 %copy.39 = f32[1,180,2880]{2,0,1:T(1,128)} copy(f32[1,180,2880]{2,1,0:T(8,128)S(1)} %bitcast.25) | data formatting | bytes 4147200
  196.5 3.5 %copy.40 = f32[1,180,2880]{2,0,1:T(1,128)} copy(f32[1,180,2880]{2,1,0:T(8,128)S(1)} %bitcast.24) | data formatting | bytes 4147200
  200.0 3.5 %copy.41 = f32[1,180,2880]{2,0,1:T(1,128)} copy(f32[1,180,2880]{2,1,0:T(8,128)S(1)} %bitcast.23) | data formatting | bytes 4147200
  203.6 0.2 fusion.8
  203.8 0.2 iota_compare_fusion
  204.0 7.6 %all-to-all-done = bf16[16,72,182]{2,1,0:T(8,128)(2,1)S(1)} async-done(((bf16[16,72,182]{2,1,0:T(8,128)(2,1)}), bf16[16,72,182]{2,1,0:T(8,128)(2,1)S(1)}, u32[]{:S(2)}, u32[]{:S(2)}) %all-to-all-start) | async-done | bytes 419360 | tf_op jit(solution)/shard_map/all_to_all | solution.py:484
  211.5 0.9 fusion.4
  212.5 0.7 slice_reduce_fusion
  213.2 0.6 copy.45
  (15 shorter events, 0.2 us)
Async XLA Ops:
  36.7 0.9 copy-start
  182.8 10.2 %copy-start.3 = (f32[180,2880]{1,0:T(8,128)S(1)}, f32[180,2880]{1,0:T(8,128)}, u32[]{:S(2)}) copy-start(f32[180,2880]{1,0:T(8,128)} %get-tuple-element.12) | copy-start | bytes 6220804
  185.1 26.4 %all-to-all-start = ((bf16[16,72,182]{2,1,0:T(8,128)(2,1)}), bf16[16,72,182]{2,1,0:T(8,128)(2,1)S(1)}, u32[]{:S(2)}, u32[]{:S(2)}) async-start(bf16[16,72,182]{2,1,0:T(8,128)(2,1)} %pad_maximum_fusion), calls=%async_computation | async-start | bytes 1179648 | tf_op jit(solution)/shard_map/all_to_all | solution.py:484
  193.0 3.5 %copy-start.2 = (f32[180,2880]{1,0:T(8,128)S(1)}, f32[180,2880]{1,0:T(8,128)}, u32[]{:S(2)}) copy-start(f32[180,2880]{1,0:T(8,128)} %get-tuple-element.13) | copy-start | bytes 6220804
  196.5 3.5 %copy-start.1 = (f32[180,2880]{1,0:T(8,128)S(1)}, f32[180,2880]{1,0:T(8,128)}, u32[]{:S(2)}) copy-start(f32[180,2880]{1,0:T(8,128)} %get-tuple-element.14) | copy-start | bytes 6220804
  200.0 3.5 %copy-start.4 = (s32[192,4]{0,1:T(4,128)S(1)}, s32[192,4]{0,1:T(4,128)}, u32[]{:S(2)}) copy-start(s32[192,4]{0,1:T(4,128)} %param.9) | copy-start | bytes 9220

commit v2 on v1

v2 whole, which is shorter than its diff:
```python
import jax
import jax.numpy as jnp
from jax import lax
from jax.experimental import pallas as pl
from jax.experimental.pallas import tpu as pltpu
from jax.sharding import Mesh
from jax.sharding import PartitionSpec as P

HIDDEN = ("hidden_0", "hidden_1")
BF = jnp.bfloat16
F32 = jnp.float32
TOK = 192
CAP = 72
NB = 16
SH = 180
ROWS = NB * CAP
W2 = 384
CH = 2 * CAP
NC = ROWS // CH
RET = 80
MESH_ID = pl.DeviceIdType.MESH
NT = (((1,), (1,)), ((), ()))
TN = (((0,), (0,)), ((), ()))


def remote(src, dst, send, recv, device):
    return pltpu.make_async_remote_copy(
        src_ref=src, dst_ref=dst, send_sem=send, recv_sem=recv,
        device_id=device, device_id_type=MESH_ID,
    )


def layer_kernel(
    x_ref, dy_ref, ids_ref, rw_ref, wg_ref, wu_ref, wd_ref,
    gg_ref, gu_ref, gd_ref, gin_ref, gr_ref,
    xin, buf, xd, wraw, wf, wb, part, fwd, near, quart, gsum, term, dgu_t, hw_t, rp, rp_all,
    ret, got, rsend, rgot, gacc, racc, grads, chosen,
    w_sem, z_send, z_recv, sib_recv, ag_send, ag_recv, rs_send, rs_recv, rt_send, rt_recv,
    ret_send, ret_recv, rr_send, rr_recv, g_sem,
):
    e = lax.axis_index("expert")
    hx, hy = lax.axis_index("hidden_0"), lax.axis_index("hidden_1")
    me = hx * 4 + hy
    z, core = e // 2, e % 2
    ef = e.astype(F32)

    def peer(j):
        return (e, j // 4, j % 4)

    def owner(j):
        return (j, hx, hy)

    barrier = pltpu.get_barrier_semaphore()
    for d in range(1, NB):
        pl.semaphore_signal(barrier, inc=1, device_id=peer((me + d) % NB), device_id_type=MESH_ID)
        pl.semaphore_signal(barrier, inc=1, device_id=owner((e + d) % NB), device_id_type=MESH_ID)
    raw = [wg_ref, wu_ref, wd_ref]
    load = [pltpu.make_async_copy(raw[k], wraw.at[k % 2], w_sem.at[k]) for k in range(3)]
    load[0].start()
    load[1].start()
    rw = rw_ref[...]
    w_hi = rw.astype(BF).astype(F32)
    xt = [x_ref[...].astype(F32), ids_ref[...].astype(F32), w_hi, rw - w_hi]
    xin[:, 0:192] = jnp.concatenate(xt, axis=0).T.astype(BF)
    yt = [dy_ref[...].astype(F32), jnp.zeros((192 - SH, TOK), F32)]
    xin[:, 192:384] = jnp.concatenate(yt, axis=0).T.astype(BF)
    pl.semaphore_wait(barrier, 2 * (NB - 1))

    right = ((z + 1) % 8) * 2 + core
    left = ((z + 7) % 8) * 2 + core
    sib = z * 2 + 1 - core
    half = TOK // 2

    def zcopy(first, h, block, target, recv):
        rows = pl.ds(half * h, half)
        src = xin.at[rows] if first else buf.at[block, rows]
        return remote(src, buf.at[block, rows], z_send.at[0], recv, owner(target))

    def zfirst():
        for h in range(2):
            zcopy(True, h, e, sib, sib_recv.at[0]).start()
        for h in range(2):
            zcopy(True, h, e, right, z_recv.at[0, 0]).start()
            zcopy(True, h, e, left, z_recv.at[0, 1]).start()

    def zwait(block, recv, n):
        at = buf.at[block, pl.ds(0, half * n)]
        remote(at, at, z_send.at[0], recv, owner(sib)).wait_recv()

    def zstage(s):
        for way in range(2):
            d = -s if way == 0 else s
            block = ((z + d + 8) % 8) * 2 + core
            zwait(block, z_recv.at[s - 1, way], 2 if s < 4 else 1)
            for h in range(2):
                if s == 4 and h != way:
                    continue
                if s < 3 or (s == 3 and h == way):
                    zcopy(False, h, block, (right, left)[way], z_recv.at[s, way]).start()
                zcopy(False, h, block, sib, sib_recv.at[s if way == 0 else 8 - s]).start()

    lane = lax.broadcasted_iota(jnp.int32, (TOK, 128), 1)
    id_lane = (lane >= 52) & (lane < 56)

    def picks(meta, expert):
        lower = (
            lax.broadcasted_iota(jnp.int32, (TOK, TOK), 0)
            > lax.broadcasted_iota(jnp.int32, (TOK, TOK), 1)
        ).astype(F32).astype(BF)
        hit = ((meta == expert) & id_lane).astype(F32).astype(BF)
        named = jnp.dot(hit, jnp.ones((128, 128), BF), preferred_element_type=F32)
        slot = jnp.dot(lower, named.astype(BF), preferred_element_type=F32)
        return ((slot == lane.astype(F32)) & (named > 0.5)).astype(F32).astype(BF)

    def rows_of(c):
        return pl.ds(pl.multiple_of(c * CH, 16), CH)

    def stage_x(c):
        plane = (z + c) % 8
        other = plane * 2 + 1 - core
        zwait(other, sib_recv.at[(8 - c) % 8], 2)
        pair = []
        for k in range(2):
            blk = buf[plane * 2 + k]
            pick = picks(blk[:, 128:256].astype(F32), ef)
            pair.append(lax.dot_general(pick, blk, TN, preferred_element_type=F32)[:CAP])
        xd[me, rows_of(c), :] = jnp.concatenate(pair, axis=0).astype(BF)

    def place(c):
        odd = c % 2
        a = jnp.where(odd == 0, hx, hy)
        b = jnp.where(odd == 0, hy, hx)
        return odd, a, b

    def shard(odd, a, b):
        return jnp.where(odd == 0, a * 4 + b, b * 4 + a)

    def ag(c, slot, to, k):
        at = xd.at[slot, rows_of(c)]
        group = 0 if k < 2 else 1 if k in (2, 3, 6, 7) else 2 if k == 10 else 3
        return remote(at, at, ag_send.at[c], ag_recv.at[c, group], peer(to))

    def ag_all(c, group, n):
        at = xd.at[pl.ds(0, n), rows_of(c)]
        return remote(at, at, ag_send.at[c], ag_recv.at[c, group], peer(me))

    def stage_a(c):
        odd, a, b = place(c)
        ag(c, me, shard(odd, (a + 1) % 4, b), 0).start()
        ag(c, me, shard(odd, (a + 3) % 4, b), 1).start()
        ag(c, me, shard(odd, a, (b + 1) % 4), 3).start()
        ag(c, me, shard(odd, a, (b + 3) % 4), 4).start()

    def stage_b(c):
        odd, a, b = place(c)
        from_left = shard(odd, (a + 3) % 4, b)
        from_right = shard(odd, (a + 1) % 4, b)
        flip = (c // 2) % 2
        ag_all(c, 0, 2).wait_recv()
        ag(
            c, jnp.where(flip == 0, from_left, from_right),
            jnp.where(flip == 0, from_right, from_left), 2,
        ).start()
        up, down = shard(odd, a, (b + 1) % 4), shard(odd, a, (b + 3) % 4)
        ag(c, from_left, up, 5).start()
        ag(c, from_left, down, 6).start()
        ag(c, from_right, up, 7).start()
        ag(c, from_right, down, 8).start()

    def stage_c(c):
        odd, a, b = place(c)
        far = shard(odd, (a + 2) % 4, b)
        up, down = shard(odd, a, (b + 1) % 4), shard(odd, a, (b + 3) % 4)
        ag_all(c, 1, 4).wait_recv()
        ag(c, far, up, 9).start()
        ag(c, far, down, 10).start()
        for k, da in ((11, 0), (12, 1)):
            slot = shard(odd, (a + da) % 4, (b + 3) % 4)
            ag(c, slot, up, k).start()
        slot = shard(odd, (a + 3) % 4, (b + 1) % 4)
        ag(c, slot, down, 13).start()

    def stage_d(c):
        odd, a, b = place(c)
        slot = shard(odd, (a + 2) % 4, (b + 1) % 4)
        ag_all(c, 2, 1).wait_recv()
        ag(c, slot, shard(odd, a, (b + 3) % 4), 14).start()

    def rs(c, src, dst, k, to):
        group = (0, 1, 2, 2, 2, 2, 3, 4, 4)[k]
        return remote(src, dst, rs_send.at[c, k // 6], rs_recv.at[c, group], peer(to))

    def rs_copy(c, k):
        odd, a, b = place(c)
        right, left = shard(odd, (a + 1) % 4, b), shard(odd, (a + 3) % 4, b)
        up, down = shard(odd, a, (b + 1) % 4), shard(odd, a, (b + 3) % 4)
        ar, al, ao = (a + 1) % 4, (a + 3) % 4, (a + 2) % 4
        bu, bd, bo = (b + 1) % 4, (b + 3) % 4, (b + 2) % 4
        if k == 0:
            return rs(c, part.at[c, ao, 0], fwd.at[c, 0], k, right)
        if k == 1:
            return rs(c, part.at[c, ao, 1], fwd.at[c, 1], k, left)
        if k == 2:
            return rs(c, part.at[c, ar, 1], near.at[c, 0, 1], k, right)
        if k == 3:
            return rs(c, part.at[c, al, 0], near.at[c, 1, 0], k, left)
        if k == 4:
            return rs(c, part.at[c, ar, 0], near.at[c, 0, 0], k, right)
        if k == 5:
            return rs(c, part.at[c, al, 1], near.at[c, 1, 1], k, left)
        flip = (c // 2) % 2
        ahead, behind = jnp.where(flip == 0, up, down), jnp.where(flip == 0, down, up)
        ba, bb = jnp.where(flip == 0, bu, bd), jnp.where(flip == 0, bd, bu)
        if k == 6:
            return rs(c, quart.at[c, bo], gsum.at[c], k, ahead)
        if k == 7:
            return rs(c, quart.at[c, bb], term.at[c, 0], k, behind)
        return rs(c, quart.at[c, ba], term.at[c, 1], k, ahead)

    def stage_e(c):
        odd, a, b = place(c)
        rows = rows_of(c)
        ag_all(c, 3, 8).wait_recv()

        gate = up = back = None
        for s in range(NB):
            x = xd[s, rows, 0:256]
            y = xd[s, rows, 128:384]
            g1 = lax.dot_general(x, wf[0, s], NT, preferred_element_type=F32)
            u1 = lax.dot_general(x, wf[1, s], NT, preferred_element_type=F32)
            b1 = lax.dot_general(y, wf[2, s], NT, preferred_element_type=F32)
            gate = g1 if gate is None else gate + g1
            up = u1 if up is None else up + u1
            back = b1 if back is None else back + b1
        meta = xd[0, rows, 128:256].astype(F32)
        lane = lax.broadcasted_iota(jnp.int32, (CH, 128), 1)
        whole = pltpu.roll(meta, 124, 1) + pltpu.roll(meta, 120, 1)
        mine = (meta == e.astype(F32)) & (lane >= 52) & (lane < 56)
        w = jnp.sum(jnp.where(mine, whole, 0.0), axis=1, keepdims=True)
        sig = jax.nn.sigmoid(gate)
        act = gate * sig
        prod = act * up
        gh = w * back
        d_gate = gh * up * sig * (1.0 + gate * (1.0 - sig))
        d_up = gh * act
        hb = prod.astype(BF).astype(F32) * back
        hi = hb.astype(BF)
        lo = (hb - hi.astype(F32)).astype(BF)
        row8 = (lax.broadcasted_iota(jnp.int32, (8, 192), 0) == c).astype(F32).astype(BF)
        rp[:, 0:CH] += lax.dot_general(
            row8, hi, NT, preferred_element_type=F32
        ) + lax.dot_general(row8, lo, NT, preferred_element_type=F32)
        dgb, dub = d_gate.astype(BF), d_up.astype(BF)
        dgu_t[c, 0:192, :] = d_gate.T.astype(BF)
        dgu_t[c, 192:384, :] = d_up.T.astype(BF)
        hw_t[c] = (w * prod).T.astype(BF)
        for q in range(4):
            for h in range(2):
                lanes = slice(768 * q + 384 * h, 768 * q + 384 * h + 384)
                p = jnp.dot(dgb, wb[odd, 0, :, lanes], preferred_element_type=F32) + jnp.dot(
                    dub, wb[odd, 1, :, lanes], preferred_element_type=F32
                )
                part[c, q, h] = p.astype(BF)
        for k in range(4):
            rs_copy(c, k).start()

    def stage_f(c):
        odd, a, b = place(c)
        ar, al = (a + 1) % 4, (a + 3) % 4
        rs_copy(c, 0).wait_recv()
        part[c, ar, 0] = (part[c, ar, 0].astype(F32) + fwd[c, 0].astype(F32)).astype(BF)
        rs_copy(c, 4).start()
        rs_copy(c, 1).wait_recv()
        part[c, al, 1] = (part[c, al, 1].astype(F32) + fwd[c, 1].astype(F32)).astype(BF)
        rs_copy(c, 5).start()

    def stage_g(c):
        odd, a, b = place(c)
        at = near.at[c]
        remote(at, at, rs_send.at[c, 0], rs_recv.at[c, 2], peer(me)).wait_recv()
        for h in range(2):
            q = (
                part[c, a, h].astype(F32) + near[c, 0, h].astype(F32) + near[c, 1, h].astype(F32)
            ).astype(BF)
            quart[c, 2 * h] = q[:, 0:256]
            quart[c, 2 * h + 1] = q[:, 128:384]
        rs_copy(c, 6).start()
        rs_copy(c, 7).start()

    def stage_h(c):
        odd, a, b = place(c)
        flip = (c // 2) % 2
        ba = jnp.where(flip == 0, (b + 1) % 4, (b + 3) % 4)
        rs_copy(c, 6).wait_recv()
        quart[c, ba] = (quart[c, ba].astype(F32) + gsum[c].astype(F32)).astype(BF)
        rs_copy(c, 8).start()

    def back_copy(c, k, src, dst, send, recv, split):
        at = src.at[c, k] if split else src.at[c]
        to = ((z + c) % 8) * 2 + k
        return remote(at, dst.at[e], send.at[0], recv.at[c if split else 0], owner(to))

    def send_back(c, src, dst, send, recv, split):
        @pl.when(c > 0)
        def _():
            back_copy(c, 0, src, dst, send, recv, split).start()
            back_copy(c, 1, src, dst, send, recv, split).start()

        @pl.when(c == 0)
        def _():
            back_copy(c, 1 - core, src, dst, send, recv, split).start()
            dst[e] = src[c, core] if split else src[c]

    def back_all(n, dst, send, recv):
        at = dst.at[pl.ds(0, n)]
        return remote(at, at, send.at[0], recv, owner(sib))

    def stage_i(c):
        odd, a, b = place(c)
        at = term.at[c]
        remote(at, at, rs_send.at[c, 1], rs_recv.at[c, 4], peer(me)).wait_recv()
        r = quart[c, b].astype(F32) + term[c, 0].astype(F32) + term[c, 1].astype(F32)
        r = jnp.where(b % 2 == 1, pltpu.roll(r, 192, 1), r)
        pad = jnp.zeros((RET - CAP, 256), F32)
        ret[c, 0] = jnp.concatenate([r[0:CAP], pad], axis=0).astype(BF)
        ret[c, 1] = jnp.concatenate([r[CAP:CH], pad], axis=0).astype(BF)
        send_back(c, ret, got, ret_send, ret_recv, True)

    def choose(first, last):
        def one(j, carry):
            chosen[j] = picks(xin[:, 128:256].astype(F32), j.astype(F32))
            return carry

        lax.fori_loop(first, last, one, 0, unroll=4)

    def stage_j(c):
        @pl.when(c > 0)
        def _():
            back_all(2, got, ret_send, ret_recv.at[c]).wait_recv()

        @pl.when(c == 0)
        def _():
            back_all(1, got, ret_send, ret_recv.at[c]).wait_recv()

        total = gacc[...]
        for k in range(2):
            j = ((z + 8 - c) % 8) * 2 + k
            total = total + jnp.dot(
                chosen[j, :, 0:RET], got[j], preferred_element_type=F32
            )
        gacc[...] = total

    def routes(c):
        meta = xin[:, 128:256].astype(F32)
        total = racc[...]
        for k in range(2):
            j = ((z + 8 - c) % 8) * 2 + k
            r = rgot[j]
            r = jnp.where(core == 1, pltpu.roll(r, 256 - CAP, 1), r)[:, 0:128]
            hi = r.astype(BF).astype(F32)
            row = lax.broadcasted_iota(jnp.int32, (8, 128), 0)
            both = jnp.where(row == 0, hi, jnp.where(row == 1, r - hi, 0.0)).astype(BF)
            value = jnp.sum(
                lax.dot_general(chosen[j], both, NT, preferred_element_type=F32),
                axis=1, keepdims=True,
            )
            total = total + jnp.where((meta == j.astype(F32)) & id_lane, value, 0.0)
        racc[...] = total

    def guard(cond, f, *args):
        @pl.when(cond)
        def _():
            with jax.named_scope(f.__name__):
                f(*args)

    def prepare(k):
        load[k].wait()
        for s in range(NB):
            w = wraw[k % 2, :, SH * s : SH * s + SH]
            at = 0 if k < 2 else 64
            wf[k, s, 0:SH, at : at + SH] = w
            if k < 2:
                t = (s % 4) * 4 + s // 4
                wb[0, k, 0:SH, 192 * s : 192 * s + SH] = w
                wb[1, k, 0:SH, 192 * t : 192 * t + SH] = w
        if k == 0:
            load[2].start()

    def drain_ag(c):
        ag_all(c, 0, 15).wait_send()

    def drain_ag(c):
        ag_all(c, 0, 15).wait_send()

    def drain_rs(c):
        at = part.at[c, pl.ds(0, 3)]
        remote(at, at, rs_send.at[c, 0], rs_recv.at[c, 0], peer(me)).wait_send()
        at = quart.at[c, pl.ds(0, 3)]
        remote(at, at, rs_send.at[c, 1], rs_recv.at[c, 0], peer(me)).wait_send()

    zfirst()
    buf[e] = xin[...]
    stage_x(0)
    stage_a(0)
    rp[...] = jnp.zeros_like(rp)
    gacc[...] = jnp.zeros_like(gacc)
    racc[...] = jnp.zeros_like(racc)
    wf[...] = jnp.zeros_like(wf)
    wb[...] = jnp.zeros_like(wb)
    prepare(0)
    stage_b(0)
    zstage(1)
    stage_x(1)
    stage_a(1)
    prepare(1)
    choose(0, 8)
    stage_c(0)
    stage_b(1)
    zstage(2)
    stage_x(2)
    stage_a(2)
    stage_d(0)
    prepare(2)
    choose(8, 16)
    zstage(3)
    stage_c(1)
    zstage(4)

    def step(t, carry):
        guard(t < NC - 1, stage_x, t + 1)
        guard(t < NC - 1, stage_a, t + 1)
        guard(t >= 2, stage_b, t)
        guard(t >= 2, stage_d, t - 1)
        guard(t >= 3, stage_f, t - 3)
        guard(t >= 2, stage_e, t - 2)
        guard(t >= 2, stage_c, t)
        guard(t >= 3, stage_g, t - 3)
        guard(t >= 4, stage_h, t - 4)
        guard(t >= 5, stage_i, t - 5)
        guard(t >= 6, stage_j, t - 6)
        guard(t >= 4, drain_ag, t - 4)
        guard(t >= 6, drain_rs, t - 6)
        return carry

    lax.fori_loop(2, NC, step, 0)

    def rt(d):
        j = (me + d) % NB
        return remote(rp, rp_all.at[me], rt_send.at[0], rt_recv.at[0], peer(j))

    def rt_all():
        at = rp_all.at[pl.ds(0, NB - 1)]
        return remote(at, at, rt_send.at[0], rt_recv.at[0], peer(me))

    def routes_out():
        for d in range(1, NB):
            rt(d).start()
        rp_all[me] = rp[...]

    def routes_back():
        rt_all().wait_recv()
        total = rp_all[0]
        for j in range(1, NB):
            total = total + rp_all[j]
        for k in range(NC):
            rsend[k] = jnp.broadcast_to(total[k : k + 1, :], (8, 256))
            send_back(k, rsend, rgot, rr_send, rr_recv, False)

    def weight_grads(s):
        gu = hd = None
        for c in range(NC):
            x = xd[s, CH * c : CH * c + CH, 0:256]
            y = xd[s, CH * c : CH * c + CH, 128:384]
            g1 = jnp.dot(dgu_t[c], x, preferred_element_type=F32)
            h1 = jnp.dot(hw_t[c], y, preferred_element_type=F32)
            gu = g1 if gu is None else gu + g1
            hd = h1 if hd is None else hd + h1
        lanes = slice(SH * s, SH * s + SH)
        grads[0, :, lanes] = gu[0:SH, 0:SH]
        grads[1, :, lanes] = gu[192 : 192 + SH, 0:SH]
        grads[2, :, lanes] = hd[0:SH, 64 : 64 + SH]

    def grad_copy(k, i):
        lanes = slice((0, 1152, 1920)[i], (1152, 1920, 2880)[i])
        out = (gg_ref, gu_ref, gd_ref)[k]
        return pltpu.make_async_copy(grads.at[k, :, lanes], out.at[:, 0, lanes], g_sem.at[k])

    def wg(first, last):
        with jax.named_scope("wg"):
            for s in range(first, last):
                weight_grads(s)

    def tail(f, c):
        with jax.named_scope(f.__name__):
            f(c)

    def grads_out(i):
        for k in range(3):
            grad_copy(k, i).start()

    tail(stage_d, 7)
    tail(stage_f, 5)
    tail(stage_e, 6)
    tail(stage_g, 5)
    tail(stage_h, 4)
    tail(stage_i, 3)
    tail(stage_j, 2)
    tail(stage_e, 7)
    routes_out()
    tail(stage_f, 6)
    drain_ag(4)
    wg(0, 4)
    tail(stage_h, 5)
    tail(stage_g, 6)
    tail(stage_f, 7)
    tail(stage_i, 4)
    tail(stage_j, 3)
    wg(4, 7)
    grads_out(0)
    tail(stage_h, 6)
    tail(stage_i, 5)
    tail(stage_j, 4)
    wg(7, 9)
    tail(stage_g, 7)
    routes_back()
    wg(9, 11)
    grads_out(1)
    tail(stage_i, 6)
    tail(stage_h, 7)
    tail(stage_j, 5)
    wg(11, 16)
    grads_out(2)
    tail(stage_i, 7)
    tail(stage_j, 6)
    back_all(NB - 1, rgot, rr_send, rr_recv.at[0]).wait_recv()
    for k in range(NC):
        tail(routes, k)
    gr_ref[...] = racc[...].T[52:56]
    with jax.named_scope("drain"):
        for k in range(5, NC):
            drain_ag(k)
        for k in range(2, NC):
            drain_rs(k)
        rt_all().wait_send()
        at = buf.at[pl.ds(0, 15)]
        remote(at, at, z_send.at[0], z_recv.at[0, 0], owner(sib)).wait_send()
        back_all(NB - 1, rgot, rr_send, rr_recv.at[0]).wait_send()
    with jax.named_scope("grads"):
        for k in range(3):
            out = (gg_ref, gu_ref, gd_ref)[k]
            pltpu.make_async_copy(grads.at[k], out.at[:, 0], g_sem.at[k]).wait()
    tail(stage_j, 7)
    back_all(NB - 1, got, ret_send, ret_recv.at[0]).wait_send()
    with jax.named_scope("gin"):
        gin_ref[...] = gacc[...].T[0:SH].astype(BF)


def layer(x, dy, ids, rw, w_gate, w_up, w_down):
    vm = pl.BlockSpec(memory_space=pltpu.VMEM)
    hbm = pl.BlockSpec(memory_space=pl.ANY)
    grad = jax.ShapeDtypeStruct((SH, 1, NB * SH), F32)
    dma = pltpu.SemaphoreType.DMA
    return pl.pallas_call(
        layer_kernel,
        out_shape=[
            grad, grad, grad,
            jax.ShapeDtypeStruct((SH, TOK), BF),
            jax.ShapeDtypeStruct((4, TOK), F32),
        ],
        in_specs=[vm] * 4 + [hbm] * 3,
        out_specs=[hbm] * 3 + [vm] * 2,
        scratch_shapes=[
            pltpu.VMEM((TOK, W2), BF),
            pltpu.VMEM((NB, TOK, W2), BF),
            pltpu.VMEM((NB, ROWS, W2), BF),
            pltpu.VMEM((2, SH, NB * SH), BF),
            pltpu.VMEM((3, NB, 192, 256), BF),
            pltpu.VMEM((2, 2, 192, NB * 192), BF),
            pltpu.VMEM((NC, 4, 2, CH, 384), BF),
            pltpu.VMEM((NC, 2, CH, 384), BF),
            pltpu.VMEM((NC, 2, 2, CH, 384), BF),
            pltpu.VMEM((NC, 4, CH, 256), BF),
            pltpu.VMEM((NC, CH, 256), BF),
            pltpu.VMEM((NC, 2, CH, 256), BF),
            pltpu.VMEM((NC, 384, CH), BF),
            pltpu.VMEM((NC, 192, CH), BF),
            pltpu.VMEM((8, 256), F32),
            pltpu.VMEM((NB, 8, 256), F32),
            pltpu.VMEM((NC, 2, RET, 256), BF),
            pltpu.VMEM((NB, RET, 256), BF),
            pltpu.VMEM((NC, 8, 256), F32),
            pltpu.VMEM((NB, 8, 256), F32),
            pltpu.VMEM((TOK, 256), F32),
            pltpu.VMEM((TOK, 128), F32),
            pltpu.VMEM((3, SH, NB * SH), F32),
            pltpu.VMEM((NB, TOK, 128), BF),
            dma((3,)),
            dma((1,)),
            dma((4, 2)),
            dma((8,)),
            dma((NC,)),
            dma((NC, 4)),
            dma((NC, 2)),
            dma((NC, 5)),
            dma((1,)),
            dma((1,)),
            dma((1,)),
            dma((NC,)),
            dma((1,)),
            dma((1,)),
            dma((3,)),
        ],
        compiler_params=pltpu.CompilerParams(
            collective_id=0, has_side_effects=True, vmem_limit_bytes=67043328
        ),
        name="layer",
    )(x, dy, ids, rw, w_gate, w_up, w_down)


def finish_kernel(g0, g1, g2, gin_ref, gr_ref, o0, o1, o2, ogin_ref, ogr_ref, held, sem):
    rows = SH // 6

    def piece(k, i, out):
        part = pl.ds(rows * i, rows)
        inner = held.at[k, part]
        outer = ((o0, o1, o2) if out else (g0, g1, g2))[k].at[part]
        src, dst = (inner, outer) if out else (outer, inner)
        return pltpu.make_async_copy(src, dst, sem.at[out, k, i])

    for k in range(3):
        for i in range(6):
            piece(k, i, 0).start()
    ogin_ref[...] = gin_ref[...]
    ogr_ref[...] = gr_ref[...]
    for k in range(3):
        for i in range(6):
            piece(k, i, 0).wait()
            piece(k, i, 1).start()
    for k in range(3):
        for i in range(6):
            piece(k, i, 1).wait()


def finish(*arrays):
    vm = pl.BlockSpec(memory_space=pltpu.VMEM)
    hbm = pl.BlockSpec(memory_space=pl.ANY)
    return pl.pallas_call(
        finish_kernel,
        out_shape=[jax.ShapeDtypeStruct(a.shape, a.dtype) for a in arrays],
        in_specs=[hbm] * 3 + [vm] * 2,
        out_specs=[hbm] * 3 + [vm] * 2,
        scratch_shapes=[
            pltpu.VMEM((3, SH, 1, NB * SH), F32),
            pltpu.SemaphoreType.DMA((2, 3, 6)),
        ],
        name="finish",
    )(*arrays)


def per_device(inputs, out_grad, expert_ids, route_weight, w_gate, w_up, w_down):
    found = layer(
        inputs.T, out_grad.T, expert_ids.T, route_weight.T, w_gate[0], w_up[0], w_down[0]
    )
    gg, gu, gd, grad_input, grad_route = finish(*found)
    grads = [jnp.transpose(g, (1, 0, 2)) for g in (gg, gu, gd)]
    return (grad_input.T, grad_route.T, *grads)


def solution(mesh):
    torus = Mesh(
        mesh.devices.reshape(mesh.shape["expert"], 4, 4), ("expert", "hidden_0", "hidden_1")
    )
    placed = (
        P("expert", HIDDEN),
        P("expert", HIDDEN),
        P("expert", None),
        P("expert", None),
        P("expert", HIDDEN, None),
        P("expert", HIDDEN, None),
        P("expert", HIDDEN, None),
    )
    return jax.shard_map(
        per_device,
        mesh=torus,
        in_specs=placed,
        out_specs=(
            P("expert", HIDDEN),
            P("expert", None),
            P("expert", HIDDEN, None),
            P("expert", HIDDEN, None),
            P("expert", HIDDEN, None),
        ),
        check_vma=False,
    )
```

time: 214 us -> 167 us (0.78)
  local copies, waits for them, and re-layouts: 15.9 us -> 0 us
  Pallas kernels: 176 us -> 165 us
  starting transfers between devices: 7.86 us -> 0 us
  waiting for transfers between devices: 7.55 us -> 0 us
  other arithmetic: 4.7 us -> 0 us
    unnamed x16 -> x0, local copies, waits for them, and re-layouts: 14 us -> none
    pallas_call x2, Pallas kernels: 176 us -> 165 us  [the longest x1 158 us: layer(): pl.pallas_call(layer_kernel, out_shape=[grad, grad, grad, jax.ShapeDtypeS...]
    all_to_all x1 -> x0, starting transfers between devices: 7.86 us -> none  [per_device(): lax.all_to_all(send, 'expert', split_axis=0, concat_axis=0, tiled=True)]
    all_to_all x1 -> x0, waiting for transfers between devices: 7.55 us -> none  [per_device(): lax.all_to_all(send, 'expert', split_axis=0, concat_axis=0, tiled=True)]
    concatenate x1 -> x0, other arithmetic: 2.33 us -> none  [per_device(): jnp.concatenate([back[:, :SH], r_hi, r_lo], axis=1).reshape(NB, CAP, SH + 2)]
  transfers between devices with their start and end apart: 1 -> 0, of which waited for: 1 -> 0; matrix products, arithmetic and copies ran while one was open for 5% -> 0% of each run, Pallas kernels for 0% -> 0%
where the time goes in v2:
time: 167 us; the launch traced here: 166 us
  Pallas kernels  165 us (99%)
    pallas_call x1, Pallas kernels, layer(): pl.pallas_call(layer_kernel, out_shape=[grad, grad, grad, jax.ShapeDtypeS...  158 us
    pallas_call x1, Pallas kernels, finish(): pl.pallas_call(finish_kernel, out_shape=[jax.ShapeDtypeStruct(a.shape, a....  7.01 us

profile of v2, /device:TPU:1, one launch (start us, length us, event | category | flops | bytes accessed | tf_op | source)
XLA Modules:
  0.0 166.2 jit_solution(17240724170915735726)
XLA Ops:
  0.6 158.3 %layer.1 = (f32[180,1,2880]{2,1,0:T(1,128)}, f32[180,1,2880]{2,1,0:T(1,128)}, f32[180,1,2880]{2,1,0:T(1,128)}, bf16[180,192]{1,0:T(8,128)(2,1)}, f32[4,192]{1,0:T(4,128)}) custom-call(bf16[180,192]{1,0:T(8,128)(2,1)} %bitcast.15, bf16[180,192]{1,0:T(8,128)(2,1)} %bitcast.16, s32[4,192]{1,0:T(4,128)} %bitcast.17, f32[4,192]{1,0:T(4,128)} %bitcast.18, ...), custom_call_target="tpu_custom_call" | custom-call | tf_op jit(solution)/shard_map/layer/pallas_call | solution.py:563
  159.0 7.0 %finish.1 = (f32[180,1,2880]{2,1,0:T(1,128)}, f32[180,1,2880]{2,1,0:T(1,128)}, f32[180,1,2880]{2,1,0:T(1,128)}, bf16[180,192]{1,0:T(8,128)(2,1)}, f32[4,192]{1,0:T(4,128)}) custom-call(f32[180,1,2880]{2,1,0:T(1,128)} %get-tuple-element.15.g0, f32[180,1,2880]{2,1,0:T(1,128)} %get-tuple-element.16.g1, f32[180,1,2880]{2,1,0:T(1,128)} %get-tuple-element.17.g2, ...), custom_call_target="tpu_custom_call" | custom-call | tf_op jit(solution)/shard_map/finish/pallas_call | solution.py:647

commit v3 on v2

--- a/solution.py
+++ b/solution.py
@@ -408,27 +408,29 @@
     wf[...] = jnp.zeros_like(wf)
     wb[...] = jnp.zeros_like(wb)
     prepare(0)
-    stage_b(0)
+    prepare(1)
     zstage(1)
     stage_x(1)
     stage_a(1)
-    prepare(1)
+    stage_b(0)
     choose(0, 8)
-    stage_c(0)
-    stage_b(1)
     zstage(2)
     stage_x(2)
     stage_a(2)
+    stage_c(0)
+    stage_b(1)
+    zstage(3)
+    stage_x(3)
+    stage_a(3)
     stage_d(0)
     prepare(2)
     choose(8, 16)
-    zstage(3)
+    zstage(4)
     stage_c(1)
-    zstage(4)
 
     def step(t, carry):
-        guard(t < NC - 1, stage_x, t + 1)
-        guard(t < NC - 1, stage_a, t + 1)
+        guard((t >= 3) & (t < NC - 1), stage_x, t + 1)
+        guard((t >= 3) & (t < NC - 1), stage_a, t + 1)
         guard(t >= 2, stage_b, t)
         guard(t >= 2, stage_d, t - 1)
         guard(t >= 3, stage_f, t - 3)
@@ -510,27 +512,28 @@
     tail(stage_f, 6)
     drain_ag(4)
     wg(0, 4)
+    tail(stage_f, 7)
     tail(stage_h, 5)
-    tail(stage_g, 6)
-    tail(stage_f, 7)
     tail(stage_i, 4)
     tail(stage_j, 3)
-    wg(4, 7)
+    wg(4, 8)
+    tail(stage_g, 6)
+    wg(8, 9)
     grads_out(0)
-    tail(stage_h, 6)
+    tail(stage_g, 7)
     tail(stage_i, 5)
-    tail(stage_j, 4)
-    wg(7, 9)
-    tail(stage_g, 7)
     routes_back()
     wg(9, 11)
     grads_out(1)
+    tail(stage_h, 6)
+    tail(stage_j, 4)
+    tail(stage_h, 7)
+    wg(11, 14)
     tail(stage_i, 6)
-    tail(stage_h, 7)
+    tail(stage_i, 7)
     tail(stage_j, 5)
-    wg(11, 16)
+    wg(14, 16)
     grads_out(2)
-    tail(stage_i, 7)
     tail(stage_j, 6)
     back_all(NB - 1, rgot, rr_send, rr_recv.at[0]).wait_recv()
     for k in range(NC):
@@ -618,27 +621,20 @@
 
 
 def finish_kernel(g0, g1, g2, gin_ref, gr_ref, o0, o1, o2, ogin_ref, ogr_ref, held, sem):
-    rows = SH // 6
-
-    def piece(k, i, out):
-        part = pl.ds(rows * i, rows)
-        inner = held.at[k, part]
-        outer = ((o0, o1, o2) if out else (g0, g1, g2))[k].at[part]
-        src, dst = (inner, outer) if out else (outer, inner)
-        return pltpu.make_async_copy(src, dst, sem.at[out, k, i])
+    def piece(k, out):
+        outer = ((o0, o1, o2) if out else (g0, g1, g2))[k]
+        src, dst = (held.at[k], outer) if out else (outer, held.at[k])
+        return pltpu.make_async_copy(src, dst, sem.at[out, k])
 
     for k in range(3):
-        for i in range(6):
-            piece(k, i, 0).start()
+        piece(k, 0).start()
     ogin_ref[...] = gin_ref[...]
     ogr_ref[...] = gr_ref[...]
     for k in range(3):
-        for i in range(6):
-            piece(k, i, 0).wait()
-            piece(k, i, 1).start()
+        piece(k, 0).wait()
+        piece(k, 1).start()
     for k in range(3):
-        for i in range(6):
-            piece(k, i, 1).wait()
+        piece(k, 1).wait()
 
 
 def finish(*arrays):
@@ -651,7 +647,7 @@
         out_specs=[hbm] * 3 + [vm] * 2,
         scratch_shapes=[
             pltpu.VMEM((3, SH, 1, NB * SH), F32),
-            pltpu.SemaphoreType.DMA((2, 3, 6)),
+            pltpu.SemaphoreType.DMA((2, 3)),
         ],
         name="finish",
     )(*arrays)

time: 167 us -> 166 us (level)
  no operation moved by 1% of the time
where the time goes in v3:
time: 166 us
  Pallas kernels  165 us (99%)
    pallas_call x1, Pallas kernels, layer(): pl.pallas_call(layer_kernel, out_shape=[grad, grad, grad, jax.ShapeDtypeS...  158 us
    pallas_call x1, Pallas kernels, finish(): pl.pallas_call(finish_kernel, out_shape=[jax.ShapeDtypeStruct(a.shape, a....  6.48 us

profile of v3, /device:TPU:1, one launch (start us, length us, event | category | flops | bytes accessed | tf_op | source)
XLA Modules:
  0.0 165.8 jit_solution(4792478607268944834)
XLA Ops:
  0.6 158.5 %layer.1 = (f32[180,1,2880]{2,1,0:T(1,128)}, f32[180,1,2880]{2,1,0:T(1,128)}, f32[180,1,2880]{2,1,0:T(1,128)}, bf16[180,192]{1,0:T(8,128)(2,1)}, f32[4,192]{1,0:T(4,128)}) custom-call(bf16[180,192]{1,0:T(8,128)(2,1)} %bitcast.15, bf16[180,192]{1,0:T(8,128)(2,1)} %bitcast.16, s32[4,192]{1,0:T(4,128)} %bitcast.17, f32[4,192]{1,0:T(4,128)} %bitcast.18, ...), custom_call_target="tpu_custom_call" | custom-call | tf_op jit(solution)/shard_map/layer/pallas_call | solution.py:566
  159.1 6.5 %finish.1 = (f32[180,1,2880]{2,1,0:T(1,128)}, f32[180,1,2880]{2,1,0:T(1,128)}, f32[180,1,2880]{2,1,0:T(1,128)}, bf16[180,192]{1,0:T(8,128)(2,1)}, f32[4,192]{1,0:T(4,128)}) custom-call(f32[180,1,2880]{2,1,0:T(1,128)} %get-tuple-element.15.g0, f32[180,1,2880]{2,1,0:T(1,128)} %get-tuple-element.16.g1, f32[180,1,2880]{2,1,0:T(1,128)} %get-tuple-element.17.g2, ...), custom_call_target="tpu_custom_call" | custom-call | tf_op jit(solution)/shard_map/finish/pallas_call | solution.py:643
